TPU v7x, 32 devices: a whole 2x2x4 slice. The times are simulated.
32 devices in a mesh: seq: 4 (over z), ctx: 8 (over y, x, core).
Axes of the slice: x: 2, y: 2, z: 4, core: 2. Of those that a mesh axis runs over, the one named last changes fastest.
Arguments:
- hidden_states: bfloat16 [4, 1024, 1024], P('seq', 'ctx'), may hold values from -6 to 6
- positions: int32 [4, 1024], P('seq'), may hold values from 0 to 1023, as said below
- gain_first: bfloat16 [1024], P(('seq', 'ctx')), may hold values from 0.25 to 1.75
- weight_query: bfloat16 [1024, 2048], P(('seq', 'ctx')), may hold values from -0.1875 to 0.1875
- key_weight_matrix: bfloat16 [1024, 1024], P(('seq', 'ctx')), may hold values from -0.1875 to 0.1875
- value_weight_matrix: bfloat16 [1024, 1024], P(('seq', 'ctx')), may hold values from -0.1875 to 0.1875
- gain_query: bfloat16 [128], P(('seq', 'ctx')), may hold values from 0.25 to 1.75
- gain_key: bfloat16 [128], P(('seq', 'ctx')), may hold values from 0.25 to 1.75
- weight_output: bfloat16 [2048, 1024], P(('seq', 'ctx')), may hold values from -2 to 2
- gain_second: bfloat16 [1024], P(('seq', 'ctx')), may hold values from 0.25 to 1.75
- weight_gate: bfloat16 [1024, 3072], P(('seq', 'ctx')), may hold values from -0.1875 to 0.1875
- weight_up: bfloat16 [1024, 3072], P(('seq', 'ctx')), may hold values from -0.1875 to 0.1875
- weight_down: bfloat16 [3072, 1024], P(('seq', 'ctx')), may hold values from -0.109375 to 0.109375
- output_cotangent: bfloat16 [4, 1024, 1024], P('seq', 'ctx'), may hold values from -6 to 6
Outputs:
- layer_output: bfloat16 [4, 1024, 1024], P('seq', 'ctx')
- hidden_gradient: float32 [4, 1024, 1024], P('seq', 'ctx')
- change_first: float32 [1024], P(('seq', 'ctx'))
- delta_query: float32 [1024, 2048], P(('seq', 'ctx'))
- delta_key: float32 [1024, 1024], P(('seq', 'ctx'))
- delta_value: float32 [1024, 1024], P(('seq', 'ctx'))
- change_query: float32 [128], P(('seq', 'ctx'))
- change_key: float32 [128], P(('seq', 'ctx'))
- delta_output: float32 [2048, 1024], P(('seq', 'ctx'))
- change_second: float32 [1024], P(('seq', 'ctx'))
- delta_gate: float32 [1024, 3072], P(('seq', 'ctx'))
- delta_up: float32 [1024, 3072], P(('seq', 'ctx'))
- delta_down: float32 [3072, 1024], P(('seq', 'ctx'))
Inputs may be any that keep to these rules, and one draw needn't show every extreme that they name: In every sequence each position 0 to 1023 occurs once; the 128 stored tokens of one device of ctx are two runs of 64 consecutive ascending positions, each run starting at a multiple of 64, and their two run numbers sum to 15.
All inputs are finite; a program needn't handle non-finite values.
Results may differ from a plain program's by a relative error of at most 0.023.
Values may be sent and summed in bfloat16 or wider, within the bound.
A program may use at most 104 MiB of HBM per device.

v0:
```python
import jax
import jax.numpy as jnp
from jax import lax
from jax.sharding import PartitionSpec as P

QUERY_HEAD_COUNT = 16
KEY_VALUE_HEADS = 8
HEAD_DIMENSION = 128
EPS = 1e-06
THETA = 1000000.0
NEGATIVE = -1e30


def inverse_root(values):
    return lax.rsqrt(jnp.mean(values * values, axis=-1, keepdims=True) + EPS)


def angles(places, head_size):
    half_size = head_size // 2
    frequency = jnp.power(THETA, -jnp.arange(half_size, dtype=jnp.float32) * (2.0 / head_size))
    phases = places.astype(jnp.float32)[:, None] * frequency[None, :]
    phases = jnp.concatenate([phases, phases], axis=-1)
    return (jnp.cos(phases), jnp.sin(phases))


def rotate(values, cosines, sines):
    half_size = values.shape[-1] // 2
    turned = jnp.concatenate([-values[..., half_size:], values[..., :half_size]], axis=-1)
    return values * cosines + turned * sines


def rotate_back(upstream, cosines, sines):
    half_size = upstream.shape[-1] // 2
    scaled = upstream * sines
    turned = jnp.concatenate([scaled[..., half_size:], -scaled[..., :half_size]], axis=-1)
    return upstream * cosines + turned


def norm_backward(normed_grad, normed, inverse):
    return inverse * (normed_grad - normed * jnp.mean(normed_grad * normed, axis=-1, keepdims=True))


def local(
    hidden_states,
    positions,
    gain_first,
    weight_query,
    key_weight_matrix,
    value_weight_matrix,
    gain_query,
    gain_key,
    weight_output,
    gain_second,
    weight_gate,
    weight_up,
    weight_down,
    output_cotangent,
):
    tokens = hidden_states.shape[1]
    sequence_length = positions.shape[1]
    head_size = HEAD_DIMENSION
    query_heads = QUERY_HEAD_COUNT
    key_head_rows = KEY_VALUE_HEADS
    group_width = query_heads // key_head_rows
    scale_factor = head_size ** (-0.5)
    key_places = positions[0]
    own_places = lax.dynamic_slice_in_dim(key_places, lax.axis_index("ctx") * tokens, tokens)
    causal_mask = key_places[None, :] <= own_places[:, None]
    cosines, sines = angles(own_places, head_size)
    cosine_heads = cosines[:, None, :]
    sine_heads = sines[:, None, :]
    residual = hidden_states[0].astype(jnp.float32)
    first_gains, query_full, key_full, value_full, query_gains, key_gains, output_full = (
        lax.all_gather(gain_first, ("seq", "ctx"), axis=0, tiled=True),
        lax.all_gather(weight_query, ("seq", "ctx"), axis=0, tiled=True),
        lax.all_gather(key_weight_matrix, ("seq", "ctx"), axis=0, tiled=True),
        lax.all_gather(value_weight_matrix, ("seq", "ctx"), axis=0, tiled=True),
        lax.all_gather(gain_query, ("seq", "ctx"), axis=0, tiled=True),
        lax.all_gather(gain_key, ("seq", "ctx"), axis=0, tiled=True),
        lax.all_gather(weight_output, ("seq", "ctx"), axis=0, tiled=True),
    )
    first_scale = first_gains.astype(jnp.float32)
    query_scale = query_gains.astype(jnp.float32)
    key_scale = key_gains.astype(jnp.float32)
    first_inverse = inverse_root(residual)
    first_normed = residual * first_inverse
    leading_input = (first_normed * first_scale).astype(jnp.bfloat16)
    query_linear = jnp.dot(leading_input, query_full, preferred_element_type=jnp.float32).reshape(
        tokens, query_heads, head_size
    )
    key_projected = jnp.dot(leading_input, key_full, preferred_element_type=jnp.float32).reshape(
        tokens, key_head_rows, head_size
    )
    value_local = jnp.dot(leading_input, value_full, preferred_element_type=jnp.float32).astype(
        jnp.bfloat16
    )
    query_inverse = inverse_root(query_linear)
    query_normed = query_linear * query_inverse
    key_inverse = inverse_root(key_projected)
    key_normed = key_projected * key_inverse
    rotary_query = rotate(query_normed * query_scale, cosine_heads, sine_heads).astype(jnp.bfloat16)
    key_rotated = rotate(key_normed * key_scale, cosine_heads, sine_heads).astype(jnp.bfloat16)
    keys_all, values_all = (
        lax.all_gather(
            key_rotated.reshape(tokens, key_head_rows * head_size), "ctx", axis=0, tiled=True
        ),
        lax.all_gather(value_local, "ctx", axis=0, tiled=True),
    )
    query_blocks = rotary_query.reshape(tokens, key_head_rows, group_width, head_size)
    key_blocks = keys_all.reshape(sequence_length, key_head_rows, head_size)
    value_blocks = values_all.reshape(sequence_length, key_head_rows, head_size)

    def head_scores(head_index):
        query_head = lax.dynamic_index_in_dim(query_blocks, head_index, 1, keepdims=False)
        key_head = lax.dynamic_index_in_dim(key_blocks, head_index, 1, keepdims=False)
        value_head = lax.dynamic_index_in_dim(value_blocks, head_index, 1, keepdims=False)
        raw_scores = (
            jnp.einsum("qgd,kd->gqk", query_head, key_head, preferred_element_type=jnp.float32)
            * scale_factor
        )
        return (
            query_head,
            key_head,
            value_head,
            jnp.where(causal_mask[None], raw_scores, NEGATIVE),
        )

    def forward_head(head_index, carry):
        outputs, log_sums = carry
        query_head, key_head, value_head, scores = head_scores(head_index)
        row_max = jnp.max(scores, axis=-1, keepdims=True)
        exponent = jnp.exp(scores - row_max)
        row_total = jnp.sum(exponent, axis=-1, keepdims=True)
        weights_low = (exponent / row_total).astype(jnp.bfloat16)
        head_output = jnp.einsum(
            "gqk,kd->qgd", weights_low, value_head, preferred_element_type=jnp.float32
        )
        log_total = row_max[..., 0] + jnp.log(row_total[..., 0])
        return (
            lax.dynamic_update_index_in_dim(outputs, head_output, head_index, 1),
            lax.dynamic_update_index_in_dim(log_sums, log_total, head_index, 0),
        )

    start_carry = (
        jnp.zeros((tokens, key_head_rows, group_width, head_size), jnp.float32),
        jnp.zeros((key_head_rows, group_width, tokens), jnp.float32),
    )
    attention, log_totals = lax.fori_loop(0, key_head_rows, forward_head, start_carry)
    attention_low = attention.reshape(tokens, query_heads * head_size).astype(jnp.bfloat16)
    middle = residual + jnp.dot(attention_low, output_full, preferred_element_type=jnp.float32)
    second_gains, gate_full, up_full, down_full = (
        lax.all_gather(gain_second, ("seq", "ctx"), axis=0, tiled=True),
        lax.all_gather(weight_gate, ("seq", "ctx"), axis=0, tiled=True),
        lax.all_gather(weight_up, ("seq", "ctx"), axis=0, tiled=True),
        lax.all_gather(weight_down, ("seq", "ctx"), axis=0, tiled=True),
    )
    second_scale = second_gains.astype(jnp.float32)
    second_inverse = inverse_root(middle)
    second_normed = middle * second_inverse
    second_input = (second_normed * second_scale).astype(jnp.bfloat16)
    gate_linear = jnp.dot(second_input, gate_full, preferred_element_type=jnp.float32)
    up_linear = jnp.dot(second_input, up_full, preferred_element_type=jnp.float32)
    sigmoid_gate = jax.nn.sigmoid(gate_linear)
    silu_gate = gate_linear * sigmoid_gate
    activation = (silu_gate * up_linear).astype(jnp.bfloat16)
    layer_output = (
        middle + jnp.dot(activation, down_full, preferred_element_type=jnp.float32)
    ).astype(jnp.bfloat16)
    gate_back, up_back, down_back = (
        lax.all_gather(weight_gate, ("seq", "ctx"), axis=0, tiled=True),
        lax.all_gather(weight_up, ("seq", "ctx"), axis=0, tiled=True),
        lax.all_gather(weight_down, ("seq", "ctx"), axis=0, tiled=True),
    )
    upstream = output_cotangent[0].astype(jnp.float32)
    upstream_low = upstream.astype(jnp.bfloat16)
    delta_down = lax.psum_scatter(
        jnp.dot(activation.T, upstream_low, preferred_element_type=jnp.float32),
        ("seq", "ctx"),
        scatter_dimension=0,
        tiled=True,
    )
    act_grad = jnp.dot(upstream_low, down_back.T, preferred_element_type=jnp.float32)
    gate_low = (
        act_grad * up_linear * sigmoid_gate * (1.0 + gate_linear * (1.0 - sigmoid_gate))
    ).astype(jnp.bfloat16)
    up_low = (act_grad * silu_gate).astype(jnp.bfloat16)
    second_input_grad = jnp.dot(
        gate_low, gate_back.T, preferred_element_type=jnp.float32
    ) + jnp.dot(up_low, up_back.T, preferred_element_type=jnp.float32)
    second_gain_term = jnp.sum(second_input_grad * second_normed, axis=0)
    middle_grad = upstream + norm_backward(
        second_input_grad * second_scale, second_normed, second_inverse
    )
    hidden_units = gate_low.shape[1]
    both_low = jnp.concatenate([gate_low, up_low], axis=1)
    both_delta = lax.psum_scatter(
        jnp.dot(second_input.T, both_low, preferred_element_type=jnp.float32),
        ("seq", "ctx"),
        scatter_dimension=0,
        tiled=True,
    )
    delta_gate = both_delta[:, :hidden_units]
    delta_up = both_delta[:, hidden_units:]
    query_back, key_back, value_back, output_back = (
        lax.all_gather(weight_query, ("seq", "ctx"), axis=0, tiled=True),
        lax.all_gather(key_weight_matrix, ("seq", "ctx"), axis=0, tiled=True),
        lax.all_gather(value_weight_matrix, ("seq", "ctx"), axis=0, tiled=True),
        lax.all_gather(weight_output, ("seq", "ctx"), axis=0, tiled=True),
    )
    middle_low = middle_grad.astype(jnp.bfloat16)
    delta_output = lax.psum_scatter(
        jnp.dot(attention_low.T, middle_low, preferred_element_type=jnp.float32),
        ("seq", "ctx"),
        scatter_dimension=0,
        tiled=True,
    )
    attention_grad = jnp.dot(middle_low, output_back.T, preferred_element_type=jnp.float32).astype(
        jnp.bfloat16
    )
    attention_grad = attention_grad.reshape(tokens, key_head_rows, group_width, head_size)

    def backward_head(head_index, carry):
        query_sums, key_sums, value_sums = carry
        query_head, key_head, value_head, scores = head_scores(head_index)
        upstream_head = lax.dynamic_index_in_dim(attention_grad, head_index, 1, keepdims=False)
        log_head = lax.dynamic_index_in_dim(log_totals, head_index, 0, keepdims=False)
        probabilities = jnp.exp(scores - log_head[..., None])
        probabilities_low = probabilities.astype(jnp.bfloat16)
        prob_grad = jnp.einsum(
            "qgd,kd->gqk", upstream_head, value_head, preferred_element_type=jnp.float32
        )
        row_inner = jnp.sum(probabilities * prob_grad, axis=-1, keepdims=True)
        score_grad = (probabilities * (prob_grad - row_inner) * scale_factor).astype(jnp.bfloat16)
        query_part = jnp.einsum(
            "gqk,kd->qgd", score_grad, key_head, preferred_element_type=jnp.float32
        )
        key_part = jnp.einsum(
            "gqk,qgd->kd", score_grad, query_head, preferred_element_type=jnp.float32
        )
        value_part = jnp.einsum(
            "gqk,qgd->kd", probabilities_low, upstream_head, preferred_element_type=jnp.float32
        )
        return (
            lax.dynamic_update_index_in_dim(query_sums, query_part, head_index, 1),
            lax.dynamic_update_index_in_dim(key_sums, key_part, head_index, 1),
            lax.dynamic_update_index_in_dim(value_sums, value_part, head_index, 1),
        )

    back_carry = (
        jnp.zeros((tokens, key_head_rows, group_width, head_size), jnp.float32),
        jnp.zeros((sequence_length, key_head_rows, head_size), jnp.float32),
        jnp.zeros((sequence_length, key_head_rows, head_size), jnp.float32),
    )
    query_sums, key_sums, value_sums = lax.fori_loop(0, key_head_rows, backward_head, back_carry)
    key_total, value_total = (
        lax.psum_scatter(
            key_sums.reshape(sequence_length, key_head_rows * head_size).astype(jnp.bfloat16),
            "ctx",
            scatter_dimension=0,
            tiled=True,
        ).astype(jnp.float32),
        lax.psum_scatter(
            value_sums.reshape(sequence_length, key_head_rows * head_size).astype(jnp.bfloat16),
            "ctx",
            scatter_dimension=0,
            tiled=True,
        ).astype(jnp.float32),
    )
    value_grad_low = value_total.astype(jnp.bfloat16)
    key_pre = rotate_back(
        key_total.reshape(tokens, key_head_rows, head_size), cosine_heads, sine_heads
    )
    key_gain_term = jnp.sum(key_pre * key_normed, axis=(0, 1))
    key_low = norm_backward(key_pre * key_scale, key_normed, key_inverse).astype(jnp.bfloat16)
    key_low = key_low.reshape(tokens, key_head_rows * head_size)
    query_pre = rotate_back(
        query_sums.reshape(tokens, query_heads, head_size), cosine_heads, sine_heads
    )
    query_gain_term = jnp.sum(query_pre * query_normed, axis=(0, 1))
    query_low = norm_backward(query_pre * query_scale, query_normed, query_inverse).astype(
        jnp.bfloat16
    )
    query_low = query_low.reshape(tokens, query_heads * head_size)
    first_input_grad = (
        jnp.dot(query_low, query_back.T, preferred_element_type=jnp.float32)
        + jnp.dot(key_low, key_back.T, preferred_element_type=jnp.float32)
        + jnp.dot(value_grad_low, value_back.T, preferred_element_type=jnp.float32)
    )
    first_gain_term = jnp.sum(first_input_grad * first_normed, axis=0)
    hidden_gradient = middle_grad + norm_backward(
        first_input_grad * first_scale, first_normed, first_inverse
    )
    query_term = jnp.dot(leading_input.T, query_low, preferred_element_type=jnp.float32)
    key_term = jnp.dot(leading_input.T, key_low, preferred_element_type=jnp.float32)
    value_term = jnp.dot(leading_input.T, value_grad_low, preferred_element_type=jnp.float32)
    change_first, delta_query, delta_key, delta_value, change_query, change_key, change_second = (
        lax.psum_scatter(first_gain_term, ("seq", "ctx"), scatter_dimension=0, tiled=True),
        lax.psum_scatter(query_term, ("seq", "ctx"), scatter_dimension=0, tiled=True),
        lax.psum_scatter(key_term, ("seq", "ctx"), scatter_dimension=0, tiled=True),
        lax.psum_scatter(value_term, ("seq", "ctx"), scatter_dimension=0, tiled=True),
        lax.psum_scatter(query_gain_term, ("seq", "ctx"), scatter_dimension=0, tiled=True),
        lax.psum_scatter(key_gain_term, ("seq", "ctx"), scatter_dimension=0, tiled=True),
        lax.psum_scatter(second_gain_term, ("seq", "ctx"), scatter_dimension=0, tiled=True),
    )
    return (
        layer_output[None],
        hidden_gradient[None],
        change_first,
        delta_query,
        delta_key,
        delta_value,
        change_query,
        change_key,
        delta_output,
        change_second,
        delta_gate,
        delta_up,
        delta_down,
    )


def solution(mesh):
    return jax.shard_map(
        local,
        mesh=mesh,
        in_specs=(
            P("seq", "ctx", None),
            P("seq", None),
            P(("seq", "ctx")),
            P(("seq", "ctx"), None),
            P(("seq", "ctx"), None),
            P(("seq", "ctx"), None),
            P(("seq", "ctx")),
            P(("seq", "ctx")),
            P(("seq", "ctx"), None),
            P(("seq", "ctx")),
            P(("seq", "ctx"), None),
            P(("seq", "ctx"), None),
            P(("seq", "ctx"), None),
            P("seq", "ctx", None),
        ),
        out_specs=(
            P("seq", "ctx", None),
            P("seq", "ctx", None),
            P(("seq", "ctx")),
            P(("seq", "ctx"), None),
            P(("seq", "ctx"), None),
            P(("seq", "ctx"), None),
            P(("seq", "ctx")),
            P(("seq", "ctx")),
            P(("seq", "ctx"), None),
            P(("seq", "ctx")),
            P(("seq", "ctx"), None),
            P(("seq", "ctx"), None),
            P(("seq", "ctx"), None),
        ),
        check_vma=False,
    )
```

profile of v0, /device:TPU:0, one launch (start us, length us, event | category | flops | bytes accessed | tf_op | source)
XLA Modules:
  0.0 1713.3 jit_solution(6148967494213294258)
XLA Ops:
  12.1 42.2 %all-reduce.9 = (bf16[1024]{0:T(1024)(128)(2,1)S(1)}, bf16[128]{0:T(256)(128)(2,1)S(1)}, bf16[128]{0:T(256)(128)(2,1)S(1)}, bf16[1024]{0:T(1024)(128)(2,1)S(1)}) all-reduce(bf16[1024]{0:T(1024)(128)(2,1)S(1)} %dynamic-update-slice, bf16[128]{0:T(256)(128)(2,1)S(1)} %dynamic-update-slice.1, ...), channel_id=1, replica_groups=mesh['seq'=4,'ctx'=8] {'seq','ctx'}, use_global_device_ids=true, to_apply=%add | all-reduce | flops 2304 | bytes 9216
  55.5 14.4 all-gather.10.cloned.1.call-done
  69.9 2.9 convolution_convert_fusion.1
  73.8 54.1 %all-gather.14.cloned.1.call-done = bf16[1024,1024]{1,0:T(8,128)(2,1)} async-done(((bf16[32,1024]{1,0:T(8,128)(2,1)}), bf16[1024,1024]{1,0:T(8,128)(2,1)}) %all-gather.14.cloned.1.call-update) | async-done | bytes 2097168 | tf_op jit(solution)/shard_map/all_gather | solution.py:76
  127.8 2.9 copy.54
  137.5 19.5 %all-gather.12.cloned.1.call-done = bf16[1024,1024]{1,0:T(8,128)(2,1)} async-done(((bf16[128,1024]{1,0:T(8,128)(2,1)}), bf16[1024,1024]{1,0:T(8,128)(2,1)}) %all-gather.12.cloned.1.call-update) | async-done | bytes 2097168 | tf_op jit(solution)/shard_map/all_gather | solution.py:107
  157.0 3.4 copy_bitcast_fusion.3
  161.0 3.0 copy.56
  164.0 23.4 %all-gather.16.cloned.1.call-done = bf16[1024,1024]{0,1:T(8,128)(2,1)} async-done(((bf16[128,1024]{0,1:T(8,128)(2,1)}), bf16[1024,1024]{0,1:T(8,128)(2,1)}) %all-gather.16.cloned.1.call-update) | async-done | bytes 2097168 | tf_op jit(solution)/shard_map/all_gather | solution.py:104
  187.4 3.9 copy.57
  191.3 60.5 %all-gather.18.cloned.1.call-done = bf16[1024,2048]{1,0:T(8,128)(2,1)} async-done(((bf16[32,2048]{1,0:T(8,128)(2,1)}), bf16[1024,2048]{1,0:T(8,128)(2,1)}) %all-gather.18.cloned.1.call-update) | async-done | bytes 4194320 | tf_op jit(solution)/shard_map/all_gather | solution.py:75
  251.9 6.4 copy.55
  258.3 3.5 multiply_reduce_fusion.3
  264.0 33.8 %while.36 = (s32[]{:T(128)}, bf16[128,8,2,128]{0,3,2,1:T(8,128)(2,1)S(1)}, f32[8,2,128]{2,1,0:T(2,128)}, bf16[1024,8,128]{0,2,1:T(8,128)(2,1)}, bf16[1024,8,128]...) while((s32[]{:T(128)}, ...), condition=%wide.region_6.7_spmd.clone.clone, body=%wide.region_3.6_spmd.clone.sunk.clone | while | flops 136445696 | bytes 4143713 | solution.py:148
  297.8 17.3 %all-gather.20.cloned.1.call-done = bf16[2048,1024]{1,0:T(8,128)(2,1)} async-done(((bf16[64,1024]{1,0:T(8,128)(2,1)}), bf16[2048,1024]{1,0:T(8,128)(2,1)}) %all-gather.20.cloned.1.call-update) | async-done | bytes 4194320 | tf_op jit(solution)/shard_map/all_gather | solution.py:80
  315.1 3.0 multiply_reduce_fusion.8
  318.3 67.6 %all-gather.22.cloned.1.call-done = bf16[1024,3072]{1,0:T(8,128)(2,1)} async-done(((bf16[32,3072]{1,0:T(8,128)(2,1)}), bf16[1024,3072]{1,0:T(8,128)(2,1)}) %all-gather.22.cloned.1.call-update) | async-done | bytes 6291472 | tf_op jit(solution)/shard_map/all_gather | solution.py:153
  386.0 5.0 fusion.115
  390.9 65.6 %all-gather.24.cloned.1.call-done = bf16[1024,3072]{1,0:T(8,128)(2,1)} async-done(((bf16[32,3072]{1,0:T(8,128)(2,1)}), bf16[1024,3072]{1,0:T(8,128)(2,1)}) %all-gather.24.cloned.1.call-update) | async-done | bytes 6291472 | tf_op jit(solution)/shard_map/all_gather | solution.py:154
  456.6 4.9 fusion.116
  461.5 65.7 %all-gather.26.cloned.1.call-done = bf16[3072,1024]{1,0:T(8,128)(2,1)} async-done(((bf16[96,1024]{1,0:T(8,128)(2,1)}), bf16[3072,1024]{1,0:T(8,128)(2,1)}) %all-gather.26.cloned.1.call-update) | async-done | bytes 6291472 | tf_op jit(solution)/shard_map/all_gather | solution.py:155
  527.2 7.0 multiply_convert_fusion
  534.2 5.6 fusion.117
  539.8 2.9 multiply_reduce_fusion.4
  546.4 81.1 %while.37 = (s32[]{:T(128)}, f32[128,8,2,128]{0,3,2,1:T(8,128)}, bf16[1024,8,128]{0,2,1:T(8,128)(2,1)}, bf16[1024,8,128]{0,2,1:T(8,128)(2,1)}, bf16[1024,8,128]{...) while((s32[]{:T(128)}, f32[128,8,2,128]{0,3,2,1:T(8,128)}, ...), condition=%wide.region_11.12_spmd.clone.clone, body=%wide.region_9.11_spmd.clone.sunk.clone | while | flops 339347968 | bytes 14166661 | solution.py:254
  561.6 2.1 fusion.198
  571.7 2.1 fusion.198
  581.9 2.1 fusion.198
  592.0 2.1 fusion.198
  602.2 2.1 fusion.198
  627.5 3.9 copy.69
  633.1 2.5 copy.71
  637.1 10.5 fusion.56
  647.6 23.6 %reduce-scatter.25.cloned.1.call-done = bf16[128,1024]{1,0:T(8,128)(2,1)} async-done(((bf16[1024,1024]{1,0:T(8,128)(2,1)}), bf16[128,1024]{1,0:T(8,128)(2,1)}) %reduce-scatter.25.cloned.1.call-update) | async-done | bytes 262160
  673.1 2.8 fusion.93
  676.0 39.7 %reduce-scatter.27.cloned.1.call-done = bf16[128,1024]{1,0:T(8,128)(2,1)} async-done(((bf16[1024,1024]{1,0:T(8,128)(2,1)}), bf16[128,1024]{1,0:T(8,128)(2,1)}) %reduce-scatter.27.cloned.1.call-update) | async-done | bytes 262160
  715.7 3.8 fusion.100
  722.2 4.6 fusion.95
  728.2 5.1 fusion.97
  734.6 7.5 fusion.85
  743.3 5.3 fusion.63
  753.0 39.4 %all-reduce.8 = (f32[1024]{0:T(1024)S(1)}, f32[128]{0:T(128)S(1)}, f32[128]{0:T(128)S(1)}, f32[1024]{0:T(1024)S(1)}) all-reduce(f32[1024]{0:T(1024)S(1)} %get-tuple-element.423, f32[128]{0:T(128)S(1)} %get-tuple-element.417, f32[128]{0:T(128)S(1)} %get-tuple-element.419, ...), channel_id=4, replica_groups=mesh['seq'=4,'ctx'=8] {'seq','ctx'}, use_global_device_ids=true, to_apply=%region_18.19.clone | all-reduce | flops 2304 | bytes 18432
  795.7 169.3 %reduce-scatter.21.cloned.1.call-done = f32[32,6144]{1,0:T(8,128)} async-done(((f32[1024,6144]{1,0:T(8,128)}), f32[32,6144]{1,0:T(8,128)}) %reduce-scatter.21.cloned.1.call-update) | async-done | bytes 786448 | tf_op jit(solution)/shard_map/reduce_scatter | solution.py:196
  967.1 143.4 %reduce-scatter.15.cloned.1.call-done = f32[32,1024]{1,0:T(8,128)} async-done(((f32[1024,1024]{1,0:T(8,128)}), f32[32,1024]{1,0:T(8,128)}) %reduce-scatter.15.cloned.1.call-update) | async-done | bytes 131088 | tf_op jit(solution)/shard_map/reduce_scatter | solution.py:299
  1110.5 141.7 %reduce-scatter.17.cloned.1.call-done = f32[32,1024]{1,0:T(8,128)} async-done(((f32[1024,1024]{1,0:T(8,128)}), f32[32,1024]{1,0:T(8,128)}) %reduce-scatter.17.cloned.1.call-update) | async-done | bytes 131088 | tf_op jit(solution)/shard_map/reduce_scatter | solution.py:300
  1252.2 148.8 %reduce-scatter.13.cloned.1.call-done = f32[32,2048]{1,0:T(8,128)} async-done(((f32[1024,2048]{1,0:T(8,128)}), f32[32,2048]{1,0:T(8,128)}) %reduce-scatter.13.cloned.1.call-update) | async-done | bytes 262160 | tf_op jit(solution)/shard_map/reduce_scatter | solution.py:298
  1400.9 148.6 %reduce-scatter.19.cloned.1.call-done = f32[64,1024]{1,0:T(8,128)} async-done(((f32[2048,1024]{1,0:T(8,128)}), f32[64,1024]{1,0:T(8,128)}) %reduce-scatter.19.cloned.1.call-update) | async-done | bytes 262160 | tf_op jit(solution)/shard_map/reduce_scatter | solution.py:211
  1549.5 157.2 %reduce-scatter.23.cloned.1.call-done = f32[96,1024]{1,0:T(8,128)} async-done(((f32[3072,1024]{1,0:T(8,128)}), f32[96,1024]{1,0:T(8,128)}) %reduce-scatter.23.cloned.1.call-update) | async-done | bytes 393232 | tf_op jit(solution)/shard_map/reduce_scatter | solution.py:176
  (276 shorter events, 145.5 us)
Async XLA Ops:
  7.2 65.7 %copy-start.29 = (s32[1,1024]{1,0:T(1,128)S(1)}, s32[1,1024]{1,0:T(1,128)}, u32[]{:S(2)}) copy-start(s32[1,1024]{1,0:T(1,128)} %param.19) | copy-start | bytes 12292
  7.2 62.7 %all-gather.10.cloned.1.call-start = ((), (), s32[]{:S(2)}) async-start(), calls=%async_computation.8 | async-start | bytes 2162688 | tf_op jit(solution)/shard_map/all_gather | solution.py:77
  7.9 119.9 %all-gather.14.cloned.1.call-start = ((), (), s32[]{:S(2)}) async-start(), calls=%async_computation.10 | async-start | bytes 2162688 | tf_op jit(solution)/shard_map/all_gather | solution.py:76
  8.7 148.3 %all-gather.12.cloned.1.call-start = ((), (), s32[]{:S(2)}) async-start(), calls=%async_computation.9 | async-start | bytes 2359296 | tf_op jit(solution)/shard_map/all_gather | solution.py:107
  55.4 202.8 %copy-start.33 = (f32[128]{0:T(128)}, f32[128]{0:T(128)S(1)}, u32[]{:S(2)}) copy-start(f32[128]{0:T(128)S(1)} %add_rsqrt_fusion.3) | copy-start | bytes 1540
  72.8 114.6 %all-gather.16.cloned.1.call-start = ((), (), s32[]{:S(2)}) async-start(), calls=%async_computation.11 | async-start | bytes 2359296 | tf_op jit(solution)/shard_map/all_gather | solution.py:104
  72.9 58.9 %copy-start.36 = (f32[128]{0:T(128)}, f32[128]{0:T(128)S(1)}, u32[]{:S(2)}) copy-start(f32[128]{0:T(128)S(1)} %convert_element_type.132) | copy-start | bytes 1540
  73.7 188.4 %copy-start.24 = (f32[128,128]{0,1:T(8,128)}, f32[128,128]{0,1:T(8,128)S(1)}, u32[]{:S(2)}) copy-start(f32[128,128]{0,1:T(8,128)S(1)} %get-tuple-element.490) | copy-start | bytes 196612
  127.8 2.9 copy-start.1
  131.6 1.6 copy-start.30
  133.2 118.6 %all-gather.18.cloned.1.call-start = ((), (), s32[]{:S(2)}) async-start(), calls=%async_computation.12 | async-start | bytes 4325376 | tf_op jit(solution)/shard_map/all_gather | solution.py:75
  133.8 181.3 %all-gather.20.cloned.1.call-start = ((), (), s32[]{:S(2)}) async-start(), calls=%async_computation.13 | async-start | bytes 4325376 | tf_op jit(solution)/shard_map/all_gather | solution.py:80
  134.4 251.5 %all-gather.22.cloned.1.call-start = ((), (), s32[]{:S(2)}) async-start(), calls=%async_computation.14 | async-start | bytes 6488064 | tf_op jit(solution)/shard_map/all_gather | solution.py:153
  135.2 321.4 %all-gather.24.cloned.1.call-start = ((), (), s32[]{:S(2)}) async-start(), calls=%async_computation.15 | async-start | bytes 6488064 | tf_op jit(solution)/shard_map/all_gather | solution.py:154
  135.9 391.2 %all-gather.26.cloned.1.call-start = ((), (), s32[]{:S(2)}) async-start(), calls=%async_computation.16 | async-start | bytes 6488064 | tf_op jit(solution)/shard_map/all_gather | solution.py:155
  136.6 534.6 %reduce-scatter.25.cloned.1.call-start = ((), (), s32[]{:S(2)}) async-start(), calls=%async_computation.23 | async-start | bytes 2359296
  136.8 125.0 %copy-start.38 = (f32[128]{0:T(128)}, f32[128]{0:T(128)S(1)}, u32[]{:S(2)}) copy-start(f32[128]{0:T(128)S(1)} %convert_element_type.135) | copy-start | bytes 1540
  157.0 3.4 copy-start.12
  297.8 20.3 %copy-start.15 = (bf16[128,8,2,128]{0,3,2,1:T(8,128)(2,1)}, bf16[128,8,2,128]{0,3,2,1:T(8,128)(2,1)S(1)}, u32[]{:S(2)}) copy-start(bf16[128,8,2,128]{0,3,2,1:T(8,128)(2,1)S(1)} %get-tuple-element.309) | copy-start | bytes 1572868
  315.1 3.1 copy-start.32
  318.2 224.6 %copy-start.6 = (f32[128,1024]{1,0:T(8,128)}, f32[128,1024]{1,0:T(8,128)S(1)}, u32[]{:S(2)}) copy-start(f32[128,1024]{1,0:T(8,128)S(1)} %get-tuple-element.496) | copy-start | bytes 1572868
  318.3 138.2 %copy-start.13 = (bf16[128,1024]{1,0:T(8,128)(2,1)}, bf16[128,1024]{1,0:T(8,128)(2,1)S(1)}, u32[]{:S(2)}) copy-start(bf16[128,1024]{1,0:T(8,128)(2,1)S(1)} %multiply_convert_fusion.5) | copy-start | bytes 786436
  390.9 136.2 %copy-start.26 = (bf16[1,128,1024]{2,1,0:T(8,128)(2,1)S(1)}, bf16[1,128,1024]{2,1,0:T(8,128)(2,1)}, u32[]{:S(2)}) copy-start(bf16[1,128,1024]{2,1,0:T(8,128)(2,1)} %param.31) | copy-start | bytes 786436
  534.2 5.6 copy-start.19
  534.2 5.6 copy-start.21
  534.2 5.6 copy-start
  539.8 3.9 copy-start.2
  631.5 1.6 copy-start.23
  631.5 84.2 %reduce-scatter.27.cloned.1.call-start = ((), (), s32[]{:S(2)}) async-start(), calls=%async_computation.24 | async-start | bytes 2359296
  635.6 1.5 copy-start.22
  635.6 329.4 %reduce-scatter.21.cloned.1.call-start = ((), (), s32[]{:S(2)}) async-start(), calls=%async_computation.21 | async-start | bytes 25952256 | tf_op jit(solution)/shard_map/reduce_scatter | solution.py:196
  647.5 24.9 %copy-start.25 = (f32[128,128]{0,1:T(8,128)S(1)}, f32[128,128]{0,1:T(8,128)}, u32[]{:S(2)}) copy-start(f32[128,128]{0,1:T(8,128)} %copy-done.24) | copy-start | bytes 196612
  647.6 25.0 %copy-start.5 = (f32[128,8,128]{0,2,1:T(8,128)S(1)}, f32[128,8,128]{0,2,1:T(8,128)}, u32[]{:S(2)}) copy-start(f32[128,8,128]{0,2,1:T(8,128)} %copy-done.4) | copy-start | bytes 1572868
  647.6 25.0 %copy-start.31 = (f32[128,8]{0,1:T(8,128)S(1)}, f32[128,8]{0,1:T(8,128)}, u32[]{:S(2)}) copy-start(f32[128,8]{0,1:T(8,128)} %copy-done.30) | copy-start | bytes 12292
  647.6 25.0 %copy-start.37 = (f32[128]{0:T(128)S(1)}, f32[128]{0:T(128)}, u32[]{:S(2)}) copy-start(f32[128]{0:T(128)} %copy-done.36) | copy-start | bytes 1540
  647.6 462.9 %reduce-scatter.15.cloned.1.call-start = ((), (), s32[]{:S(2)}) async-start(), calls=%async_computation.18 | async-start | bytes 4325376 | tf_op jit(solution)/shard_map/reduce_scatter | solution.py:299
  676.0 576.2 %reduce-scatter.17.cloned.1.call-start = ((), (), s32[]{:S(2)}) async-start(), calls=%async_computation.19 | async-start | bytes 4325376 | tf_op jit(solution)/shard_map/reduce_scatter | solution.py:300
  719.5 1.2 copy-start.17
  719.5 681.4 %reduce-scatter.13.cloned.1.call-start = ((), (), s32[]{:S(2)}) async-start(), calls=%async_computation.17 | async-start | bytes 8650752 | tf_op jit(solution)/shard_map/reduce_scatter | solution.py:298
  726.8 1.5 copy-start.16
  726.8 822.7 %reduce-scatter.19.cloned.1.call-start = ((), (), s32[]{:S(2)}) async-start(), calls=%async_computation.20 | async-start | bytes 8650752 | tf_op jit(solution)/shard_map/reduce_scatter | solution.py:211
  733.3 1.3 copy-start.27
  733.3 973.4 %reduce-scatter.23.cloned.1.call-start = ((), (), s32[]{:S(2)}) async-start(), calls=%async_computation.22 | async-start | bytes 12976128 | tf_op jit(solution)/shard_map/reduce_scatter | solution.py:176
  743.3 5.3 copy-start.10
  743.3 5.3 copy-start.28
  743.3 6.2 copy-start.11
  748.6 2.7 copy-start.3
  751.3 1.7 copy-start.35
  (10 other events, 9.2 us)
Sparse Core Ops, SparseCore 0:
  10.9 58.9 all-gather.9
  72.7 55.0 all-gather.13
  130.3 26.6 all-gather.11
  159.3 28.0 all-gather.15
  190.1 61.7 all-gather.17
  254.6 60.5 all-gather.19
  318.0 67.9 all-gather.21
  388.8 67.6 all-gather.23
  459.4 67.6 all-gather.25
  631.6 39.6 reduce-scatter.24
  674.6 41.0 reduce-scatter.26
  722.0 243.0 reduce-scatter.20
  967.9 142.5 reduce-scatter.14
  1113.2 138.9 reduce-scatter.16
  1254.9 145.9 reduce-scatter.12
  1403.7 145.8 reduce-scatter.18
  1556.0 150.7 reduce-scatter.22
where the time goes:
time: 1720 us; the launch traced here: 1710 us
  waiting for transfers between devices  1370 us (80%)
  matrix products  163 us (9%)
  blocking collectives  81.5 us (5%)
  local copies, waits for them, and re-layouts  61.5 us (4%)
  other arithmetic  26.8 us (2%)
    reduce_scatter x1, waiting for transfers between devices, local(): lax.psum_scatter(jnp.dot(second_input.T, both_low, preferred_element_type...  169 us
    reduce_scatter x1, waiting for transfers between devices, local(): lax.psum_scatter(jnp.dot(activation.T, upstream_low, preferred_element_ty...  157 us
    reduce_scatter x1, waiting for transfers between devices, local(): lax.psum_scatter(query_term, ('seq', 'ctx'), scatter_dimension=0, tiled=T...  149 us
    reduce_scatter x1, waiting for transfers between devices, local(): lax.psum_scatter(jnp.dot(attention_low.T, middle_low, preferred_element_t...  149 us
    reduce_scatter x1, waiting for transfers between devices, local(): lax.psum_scatter(key_term, ('seq', 'ctx'), scatter_dimension=0, tiled=True)  143 us
    reduce_scatter x1, waiting for transfers between devices, local(): lax.psum_scatter(value_term, ('seq', 'ctx'), scatter_dimension=0, tiled=T...  142 us
    unnamed x2, blocking collectives  81.5 us
    unnamed x19, waiting for transfers between devices  68 us
  transfers between devices with their start and end apart: 17, of which 17 were waited for; matrix products, arithmetic and copies ran while one was open for 8% of the time, Pallas kernels for 0%

commit v1 on v0

--- a/solution.py
+++ b/solution.py
@@ -150,7 +150,12 @@
     middle = residual + jnp.dot(attention_low, output_full, preferred_element_type=jnp.float32)
     second_gains, gate_full, up_full, down_full = (
         lax.all_gather(gain_second, ("seq", "ctx"), axis=0, tiled=True),
-        lax.all_gather(weight_gate, ("seq", "ctx"), axis=0, tiled=True),
+        jnp.concatenate(
+            lax.all_to_all(
+                jnp.stack([weight_gate] * lax.axis_size(("seq", "ctx"))), ("seq", "ctx"), 0, 0
+            ),
+            axis=0,
+        ),
         lax.all_gather(weight_up, ("seq", "ctx"), axis=0, tiled=True),
         lax.all_gather(weight_down, ("seq", "ctx"), axis=0, tiled=True),
     )

time: 1720 us -> 1770 us (1.029)
  waiting for transfers between devices: 1370 us -> 1410 us
    all_gather x1, waiting for transfers between devices: 23.4 us -> 48.6 us  [local(): lax.all_gather(key_rotated.reshape(tokens, key_head_rows * head_size), 'c...]
    unnamed x102 -> x104, local copies, waits for them, and re-layouts: 36.4 us -> 36.4 us
  transfers between devices with their start and end apart: 17 -> 18, of which waited for: 17 -> 17; matrix products, arithmetic and copies ran while one was open for 8% -> 8% of each run, Pallas kernels for 0% -> 0%
where the time goes in v1:
time: 1770 us
  waiting for transfers between devices  1410 us (80%)
  matrix products  162 us (9%)
  blocking collectives  81.6 us (5%)
  local copies, waits for them, and re-layouts  65 us (4%)
  other arithmetic  26.8 us (2%)
    reduce_scatter x1, waiting for transfers between devices, local(): lax.psum_scatter(jnp.dot(second_input.T, both_low, preferred_element_type...  169 us
    reduce_scatter x1, waiting for transfers between devices, local(): lax.psum_scatter(jnp.dot(activation.T, upstream_low, preferred_element_ty...  157 us
    reduce_scatter x1, waiting for transfers between devices, local(): lax.psum_scatter(query_term, ('seq', 'ctx'), scatter_dimension=0, tiled=T...  149 us
    reduce_scatter x1, waiting for transfers between devices, local(): lax.psum_scatter(jnp.dot(attention_low.T, middle_low, preferred_element_t...  149 us
    reduce_scatter x1, waiting for transfers between devices, local(): lax.psum_scatter(key_term, ('seq', 'ctx'), scatter_dimension=0, tiled=True)  143 us
    reduce_scatter x1, waiting for transfers between devices, local(): lax.psum_scatter(value_term, ('seq', 'ctx'), scatter_dimension=0, tiled=T...  142 us
    unnamed x2, blocking collectives  81.6 us
    all_gather x1, waiting for transfers between devices, local(): lax.all_gather(weight_query, ('seq', 'ctx'), axis=0, tiled=True)  72.3 us
  transfers between devices with their start and end apart: 18, of which 17 were waited for; matrix products, arithmetic and copies ran while one was open for 8% of the time, Pallas kernels for 0%

profile of v1, /device:TPU:0, one launch (start us, length us, event | category | flops | bytes accessed | tf_op | source)
XLA Modules:
  0.0 1767.1 jit_solution(12413437650613683897)
XLA Ops:
  12.1 42.2 %all-reduce.9 = (bf16[1024]{0:T(1024)(128)(2,1)S(1)}, bf16[128]{0:T(256)(128)(2,1)S(1)}, bf16[128]{0:T(256)(128)(2,1)S(1)}, bf16[1024]{0:T(1024)(128)(2,1)S(1)}) all-reduce(bf16[1024]{0:T(1024)(128)(2,1)S(1)} %dynamic-update-slice, bf16[128]{0:T(256)(128)(2,1)S(1)} %dynamic-update-slice.1, ...), channel_id=1, replica_groups=mesh['seq'=4,'ctx'=8] {'seq','ctx'}, use_global_device_ids=true, to_apply=%add | all-reduce | flops 2304 | bytes 9216
  55.5 14.4 all-gather.10.cloned.1.call-done
  69.9 2.9 convolution_convert_fusion.1
  73.8 54.1 %all-gather.14.cloned.1.call-done = bf16[1024,1024]{1,0:T(8,128)(2,1)} async-done(((bf16[32,1024]{1,0:T(8,128)(2,1)}), bf16[1024,1024]{1,0:T(8,128)(2,1)}) %all-gather.14.cloned.1.call-update) | async-done | bytes 2097168 | tf_op jit(solution)/shard_map/all_gather | solution.py:76
  127.8 2.9 copy.54
  135.9 3.4 stack.2
  139.4 3.6 all-to-all-start
  144.5 36.6 %all-gather.12.cloned.1.call-done = bf16[1024,1024]{1,0:T(8,128)(2,1)} async-done(((bf16[128,1024]{1,0:T(8,128)(2,1)}), bf16[1024,1024]{1,0:T(8,128)(2,1)}) %all-gather.12.cloned.1.call-update) | async-done | bytes 2097168 | tf_op jit(solution)/shard_map/all_gather | solution.py:107
  181.2 2.2 copy.91
  183.4 3.0 copy.56
  186.4 48.6 %all-gather.16.cloned.1.call-done = bf16[1024,1024]{0,1:T(8,128)(2,1)} async-done(((bf16[128,1024]{0,1:T(8,128)(2,1)}), bf16[1024,1024]{0,1:T(8,128)(2,1)}) %all-gather.16.cloned.1.call-update) | async-done | bytes 2097168 | tf_op jit(solution)/shard_map/all_gather | solution.py:104
  235.0 4.1 copy.57
  240.8 72.3 %all-gather.18.cloned.1.call-done = bf16[1024,2048]{1,0:T(8,128)(2,1)} async-done(((bf16[32,2048]{1,0:T(8,128)(2,1)}), bf16[1024,2048]{1,0:T(8,128)(2,1)}) %all-gather.18.cloned.1.call-update) | async-done | bytes 4194320 | tf_op jit(solution)/shard_map/all_gather | solution.py:75
  313.1 6.4 copy.55
  319.5 3.5 multiply_reduce_fusion.3
  325.3 33.8 %while.36 = (s32[]{:T(128)}, bf16[128,8,2,128]{0,3,2,1:T(8,128)(2,1)S(1)}, f32[8,2,128]{2,1,0:T(2,128)}, bf16[1024,8,128]{0,2,1:T(8,128)(2,1)}, bf16[1024,8,128]...) while((s32[]{:T(128)}, ...), condition=%wide.region_6.7_spmd.clone.clone, body=%wide.region_3.6_spmd.clone.sunk.clone | while | flops 136445696 | bytes 4143713 | solution.py:148
  359.1 17.3 all-gather.20.cloned.1.call-done
  376.4 3.0 multiply_reduce_fusion.8
  379.6 5.0 fusion.115
  384.6 62.6 %all-gather.22.cloned.1.call-done = bf16[1024,3072]{1,0:T(8,128)(2,1)} async-done(((bf16[32,3072]{1,0:T(8,128)(2,1)}), bf16[1024,3072]{1,0:T(8,128)(2,1)}) %all-gather.22.cloned.1.call-update) | async-done | bytes 6291472 | tf_op jit(solution)/shard_map/all_gather | solution.py:159
  447.2 5.0 fusion.116
  452.2 65.6 %all-gather.24.cloned.1.call-done = bf16[3072,1024]{1,0:T(8,128)(2,1)} async-done(((bf16[96,1024]{1,0:T(8,128)(2,1)}), bf16[3072,1024]{1,0:T(8,128)(2,1)}) %all-gather.24.cloned.1.call-update) | async-done | bytes 6291472 | tf_op jit(solution)/shard_map/all_gather | solution.py:160
  517.8 7.1 multiply_convert_fusion
  524.9 63.5 %all-gather.26.cloned.1.call-done = bf16[1024,3072]{1,0:T(8,128)(2,1)} async-done(((bf16[32,3072]{1,0:T(8,128)(2,1)}), bf16[1024,3072]{1,0:T(8,128)(2,1)}) %all-gather.26.cloned.1.call-update) | async-done | bytes 6291472 | tf_op jit(solution)/shard_map/all_gather | solution.py:175
  588.4 5.1 fusion.117
  593.6 2.9 multiply_reduce_fusion.4
  600.3 81.0 %while.37 = (s32[]{:T(128)}, f32[128,8,2,128]{0,3,2,1:T(8,128)}, bf16[1024,8,128]{0,2,1:T(8,128)(2,1)}, bf16[1024,8,128]{0,2,1:T(8,128)(2,1)}, bf16[1024,8,128]{...) while((s32[]{:T(128)}, f32[128,8,2,128]{0,3,2,1:T(8,128)}, ...), condition=%wide.region_11.12_spmd.clone.clone, body=%wide.region_9.11_spmd.clone.sunk.clone | while | flops 339347968 | bytes 14166661 | solution.py:259
  605.3 2.1 fusion.198
  615.4 2.1 fusion.198
  676.2 2.1 fusion.198
  681.3 3.9 copy.69
  686.8 2.5 copy.71
  690.8 10.4 fusion.56
  701.4 23.7 %reduce-scatter.25.cloned.1.call-done = bf16[128,1024]{1,0:T(8,128)(2,1)} async-done(((bf16[1024,1024]{1,0:T(8,128)(2,1)}), bf16[128,1024]{1,0:T(8,128)(2,1)}) %reduce-scatter.25.cloned.1.call-update) | async-done | bytes 262160
  726.9 2.8 fusion.93
  729.8 39.7 %reduce-scatter.27.cloned.1.call-done = bf16[128,1024]{1,0:T(8,128)(2,1)} async-done(((bf16[1024,1024]{1,0:T(8,128)(2,1)}), bf16[128,1024]{1,0:T(8,128)(2,1)}) %reduce-scatter.27.cloned.1.call-update) | async-done | bytes 262160
  769.5 3.8 fusion.100
  775.9 4.6 fusion.95
  781.9 5.1 fusion.97
  788.4 7.5 fusion.85
  797.0 5.3 fusion.63
  806.8 39.4 %all-reduce.8 = (f32[1024]{0:T(1024)S(1)}, f32[128]{0:T(128)S(1)}, f32[128]{0:T(128)S(1)}, f32[1024]{0:T(1024)S(1)}) all-reduce(f32[1024]{0:T(1024)S(1)} %get-tuple-element.423, f32[128]{0:T(128)S(1)} %get-tuple-element.417, f32[128]{0:T(128)S(1)} %get-tuple-element.419, ...), channel_id=4, replica_groups=mesh['seq'=4,'ctx'=8] {'seq','ctx'}, use_global_device_ids=true, to_apply=%region_18.19.clone | all-reduce | flops 2304 | bytes 18432
  849.5 169.3 %reduce-scatter.21.cloned.1.call-done = f32[32,6144]{1,0:T(8,128)} async-done(((f32[1024,6144]{1,0:T(8,128)}), f32[32,6144]{1,0:T(8,128)}) %reduce-scatter.21.cloned.1.call-update) | async-done | bytes 786448 | tf_op jit(solution)/shard_map/reduce_scatter | solution.py:201
  1020.9 143.4 %reduce-scatter.15.cloned.1.call-done = f32[32,1024]{1,0:T(8,128)} async-done(((f32[1024,1024]{1,0:T(8,128)}), f32[32,1024]{1,0:T(8,128)}) %reduce-scatter.15.cloned.1.call-update) | async-done | bytes 131088 | tf_op jit(solution)/shard_map/reduce_scatter | solution.py:304
  1164.2 141.6 %reduce-scatter.17.cloned.1.call-done = f32[32,1024]{1,0:T(8,128)} async-done(((f32[1024,1024]{1,0:T(8,128)}), f32[32,1024]{1,0:T(8,128)}) %reduce-scatter.17.cloned.1.call-update) | async-done | bytes 131088 | tf_op jit(solution)/shard_map/reduce_scatter | solution.py:305
  1305.9 149.0 %reduce-scatter.13.cloned.1.call-done = f32[32,2048]{1,0:T(8,128)} async-done(((f32[1024,2048]{1,0:T(8,128)}), f32[32,2048]{1,0:T(8,128)}) %reduce-scatter.13.cloned.1.call-update) | async-done | bytes 262160 | tf_op jit(solution)/shard_map/reduce_scatter | solution.py:303
  1454.8 148.6 %reduce-scatter.19.cloned.1.call-done = f32[64,1024]{1,0:T(8,128)} async-done(((f32[2048,1024]{1,0:T(8,128)}), f32[64,1024]{1,0:T(8,128)}) %reduce-scatter.19.cloned.1.call-update) | async-done | bytes 262160 | tf_op jit(solution)/shard_map/reduce_scatter | solution.py:216
  1603.4 157.1 %reduce-scatter.23.cloned.1.call-done = f32[96,1024]{1,0:T(8,128)} async-done(((f32[3072,1024]{1,0:T(8,128)}), f32[96,1024]{1,0:T(8,128)}) %reduce-scatter.23.cloned.1.call-update) | async-done | bytes 393232 | tf_op jit(solution)/shard_map/reduce_scatter | solution.py:181
  (281 shorter events, 150.6 us)
Async XLA Ops:
  7.2 65.7 %copy-start.30 = (s32[1,1024]{1,0:T(1,128)S(1)}, s32[1,1024]{1,0:T(1,128)}, u32[]{:S(2)}) copy-start(s32[1,1024]{1,0:T(1,128)} %param.19) | copy-start | bytes 12292
  7.2 62.7 %all-gather.10.cloned.1.call-start = ((), (), s32[]{:S(2)}) async-start(), calls=%async_computation.9 | async-start | bytes 2162688 | tf_op jit(solution)/shard_map/all_gather | solution.py:77
  7.9 119.9 %all-gather.14.cloned.1.call-start = ((), (), s32[]{:S(2)}) async-start(), calls=%async_computation.11 | async-start | bytes 2162688 | tf_op jit(solution)/shard_map/all_gather | solution.py:76
  8.7 172.5 %all-gather.12.cloned.1.call-start = ((), (), s32[]{:S(2)}) async-start(), calls=%async_computation.10 | async-start | bytes 2359296 | tf_op jit(solution)/shard_map/all_gather | solution.py:107
  55.5 264.1 %copy-start.34 = (f32[128]{0:T(128)}, f32[128]{0:T(128)S(1)}, u32[]{:S(2)}) copy-start(f32[128]{0:T(128)S(1)} %add_rsqrt_fusion.3) | copy-start | bytes 1540
  72.8 162.1 %all-gather.16.cloned.1.call-start = ((), (), s32[]{:S(2)}) async-start(), calls=%async_computation.12 | async-start | bytes 2359296 | tf_op jit(solution)/shard_map/all_gather | solution.py:104
  72.9 58.9 %copy-start.37 = (f32[128]{0:T(128)}, f32[128]{0:T(128)S(1)}, u32[]{:S(2)}) copy-start(f32[128]{0:T(128)S(1)} %convert_element_type.132) | copy-start | bytes 1540
  73.7 249.7 %copy-start.24 = (f32[128,128]{0,1:T(8,128)}, f32[128,128]{0,1:T(8,128)S(1)}, u32[]{:S(2)}) copy-start(f32[128,128]{0,1:T(8,128)S(1)} %get-tuple-element.490) | copy-start | bytes 196612
  127.8 2.9 copy-start.1
  131.6 3.6 copy-start.31
  131.6 4.3 copy-start.29
  133.2 179.9 %all-gather.18.cloned.1.call-start = ((), (), s32[]{:S(2)}) async-start(), calls=%async_computation.13 | async-start | bytes 4325376 | tf_op jit(solution)/shard_map/all_gather | solution.py:75
  133.8 242.5 %all-gather.20.cloned.1.call-start = ((), (), s32[]{:S(2)}) async-start(), calls=%async_computation.14 | async-start | bytes 4325376 | tf_op jit(solution)/shard_map/all_gather | solution.py:80
  134.4 312.8 %all-gather.22.cloned.1.call-start = ((), (), s32[]{:S(2)}) async-start(), calls=%async_computation.15 | async-start | bytes 6488064 | tf_op jit(solution)/shard_map/all_gather | solution.py:159
  135.2 382.6 %all-gather.24.cloned.1.call-start = ((), (), s32[]{:S(2)}) async-start(), calls=%async_computation.16 | async-start | bytes 6488064 | tf_op jit(solution)/shard_map/all_gather | solution.py:160
  139.4 240.2 %all-to-all-start = ((bf16[32,32,3072]{2,1,0:T(8,128)(2,1)}), bf16[32,32,3072]{2,1,0:T(8,128)(2,1)}, u32[]{:S(2)}, u32[]{:S(2)}) async-start(bf16[32,32,3072]{2,1,0:T(8,128)(2,1)} %stack.2), calls=%async_computation | async-start | bytes 12582912 | tf_op jit(solution)/shard_map/all_to_all | solution.py:154
  143.0 445.4 %all-gather.26.cloned.1.call-start = ((), (), s32[]{:S(2)}) async-start(), calls=%async_computation.17 | async-start | bytes 6488064 | tf_op jit(solution)/shard_map/all_gather | solution.py:175
  143.7 581.3 %reduce-scatter.25.cloned.1.call-start = ((), (), s32[]{:S(2)}) async-start(), calls=%async_computation.24 | async-start | bytes 2359296
  143.8 179.3 %copy-start.39 = (f32[128]{0:T(128)}, f32[128]{0:T(128)S(1)}, u32[]{:S(2)}) copy-start(f32[128]{0:T(128)S(1)} %convert_element_type.135) | copy-start | bytes 1540
  235.0 4.1 copy-start.12
  359.1 20.3 %copy-start.15 = (bf16[128,8,2,128]{0,3,2,1:T(8,128)(2,1)}, bf16[128,8,2,128]{0,3,2,1:T(8,128)(2,1)S(1)}, u32[]{:S(2)}) copy-start(bf16[128,8,2,128]{0,3,2,1:T(8,128)(2,1)S(1)} %get-tuple-element.309) | copy-start | bytes 1572868
  376.4 3.1 copy-start.33
  379.4 217.1 %copy-start.6 = (f32[128,1024]{1,0:T(8,128)}, f32[128,1024]{1,0:T(8,128)S(1)}, u32[]{:S(2)}) copy-start(f32[128,1024]{1,0:T(8,128)S(1)} %get-tuple-element.496) | copy-start | bytes 1572868
  379.5 67.7 %copy-start.13 = (bf16[128,1024]{1,0:T(8,128)(2,1)}, bf16[128,1024]{1,0:T(8,128)(2,1)S(1)}, u32[]{:S(2)}) copy-start(bf16[128,1024]{1,0:T(8,128)(2,1)S(1)} %multiply_convert_fusion.5) | copy-start | bytes 786436
  524.9 68.6 %copy-start.19 = (bf16[128,3072]{1,0:T(8,128)(2,1)}, bf16[128,3072]{1,0:T(8,128)(2,1)S(1)}, u32[]{:S(2)}) copy-start(bf16[128,3072]{1,0:T(8,128)(2,1)S(1)} %get-tuple-element.477) | copy-start | bytes 2359300
  524.9 68.6 %copy-start.21 = (bf16[128,3072]{1,0:T(8,128)(2,1)}, bf16[128,3072]{1,0:T(8,128)(2,1)S(1)}, u32[]{:S(2)}) copy-start(bf16[128,3072]{1,0:T(8,128)(2,1)S(1)} %get-tuple-element.476) | copy-start | bytes 2359300
  588.4 5.2 copy-start
  593.6 3.0 copy-start.26
  593.6 4.0 copy-start.2
  685.2 1.6 copy-start.23
  685.2 84.2 %reduce-scatter.27.cloned.1.call-start = ((), (), s32[]{:S(2)}) async-start(), calls=%async_computation.25 | async-start | bytes 2359296
  689.3 1.5 copy-start.22
  689.4 329.5 %reduce-scatter.21.cloned.1.call-start = ((), (), s32[]{:S(2)}) async-start(), calls=%async_computation.22 | async-start | bytes 25952256 | tf_op jit(solution)/shard_map/reduce_scatter | solution.py:201
  701.2 24.9 %copy-start.25 = (f32[128,128]{0,1:T(8,128)S(1)}, f32[128,128]{0,1:T(8,128)}, u32[]{:S(2)}) copy-start(f32[128,128]{0,1:T(8,128)} %copy-done.24) | copy-start | bytes 196612
  701.3 25.0 %copy-start.5 = (f32[128,8,128]{0,2,1:T(8,128)S(1)}, f32[128,8,128]{0,2,1:T(8,128)}, u32[]{:S(2)}) copy-start(f32[128,8,128]{0,2,1:T(8,128)} %copy-done.4) | copy-start | bytes 1572868
  701.3 25.0 %copy-start.32 = (f32[128,8]{0,1:T(8,128)S(1)}, f32[128,8]{0,1:T(8,128)}, u32[]{:S(2)}) copy-start(f32[128,8]{0,1:T(8,128)} %copy-done.31) | copy-start | bytes 12292
  701.3 25.0 %copy-start.38 = (f32[128]{0:T(128)S(1)}, f32[128]{0:T(128)}, u32[]{:S(2)}) copy-start(f32[128]{0:T(128)} %copy-done.37) | copy-start | bytes 1540
  701.3 462.9 %reduce-scatter.15.cloned.1.call-start = ((), (), s32[]{:S(2)}) async-start(), calls=%async_computation.19 | async-start | bytes 4325376 | tf_op jit(solution)/shard_map/reduce_scatter | solution.py:304
  729.7 576.1 %reduce-scatter.17.cloned.1.call-start = ((), (), s32[]{:S(2)}) async-start(), calls=%async_computation.20 | async-start | bytes 4325376 | tf_op jit(solution)/shard_map/reduce_scatter | solution.py:305
  773.3 681.6 %reduce-scatter.13.cloned.1.call-start = ((), (), s32[]{:S(2)}) async-start(), calls=%async_computation.18 | async-start | bytes 8650752 | tf_op jit(solution)/shard_map/reduce_scatter | solution.py:303
  780.5 1.4 copy-start.16
  780.5 822.9 %reduce-scatter.19.cloned.1.call-start = ((), (), s32[]{:S(2)}) async-start(), calls=%async_computation.21 | async-start | bytes 8650752 | tf_op jit(solution)/shard_map/reduce_scatter | solution.py:216
  787.1 973.5 %reduce-scatter.23.cloned.1.call-start = ((), (), s32[]{:S(2)}) async-start(), calls=%async_computation.23 | async-start | bytes 12976128 | tf_op jit(solution)/shard_map/reduce_scatter | solution.py:181
  797.0 5.3 copy-start.10
  797.0 5.3 copy-start.28
  797.0 6.2 copy-start.11
  802.3 2.7 copy-start.3
  805.1 1.7 copy-start.36
  (12 other events, 11.8 us)
Sparse Core Ops, SparseCore 0:
  10.9 58.9 all-gather.9
  72.7 55.0 all-gather.13
  130.3 50.8 all-gather.11
  183.5 51.4 all-gather.15
  237.7 75.3 all-gather.17
  315.8 60.5 all-gather.19
  379.2 67.9 all-gather.21
  450.1 67.6 all-gather.23
  520.7 67.6 all-gather.25
  685.4 39.6 reduce-scatter.24
  728.3 41.0 reduce-scatter.26
  775.7 243.0 reduce-scatter.20
  1021.7 142.5 reduce-scatter.14
  1166.9 138.8 reduce-scatter.16
  1308.6 146.1 reduce-scatter.12
  1457.5 145.8 reduce-scatter.18
  1609.9 150.6 reduce-scatter.22
